TPU v7x, 256 devices: a whole 4x4x8 slice. The times are simulated.
256 devices in a mesh: blk: 128 (over z, y_lo, x, core), feat: 2 (over y_hi).
Axes of the slice: x: 4, y: 4 (y_hi: 2, y_lo: 2; y = y_hi * 2 + y_lo), z: 8, core: 2. Of those that a mesh axis runs over, the one named last changes fastest.
Arguments:
- samples: float32 [98304, 2048], P('blk', 'feat'), may hold values from -6 to 6
Outputs:
- band: float32 [5, 98304, 768], P(None, 'blk', 'feat')
All inputs are finite; a program needn't handle non-finite values.
Results may differ from a plain program's by a relative error of at most 0.0001.
Values sent between devices are 32-bit elements; how exact they have to be, the bound alone decides.
A program may use at most 128 MiB of HBM per device.

v0:
```python
import jax
import jax.numpy as jnp
from jax import lax
from jax.sharding import PartitionSpec as P


def copy_for_each(array, axis):
    copies = jnp.broadcast_to(array, (lax.axis_size(axis), *array.shape))
    return lax.all_to_all(copies, axis, split_axis=0, concat_axis=0, tiled=True)


def in_order(tiles, dim):
    tiles = jnp.moveaxis(tiles, 0, dim)
    shape = tiles.shape
    return tiles.reshape(*shape[:dim], shape[dim] * shape[dim + 1], *shape[dim + 2 :])


def gathered_copies(array, axis, dim):
    tiles = copy_for_each(array, axis)
    return in_order(tiles, dim)


def from_behind(array, axis, by):
    count = lax.axis_size(axis)
    return lax.ppermute(array, axis, [(i, (i + by) % count) for i in range(count)])


def gram_block(left, right):
    return lax.dot_general(
        left,
        right,
        (((1,), (1,)), ((), ())),
        precision=lax.Precision.HIGHEST,
        preferred_element_type=jnp.float32,
    )


def local(samples):
    width = samples.shape[1] * lax.axis_size("feat")
    scale = 1.0 / jnp.sqrt(jnp.float32(width))
    full = gathered_copies(samples, "feat", 1)
    columns = samples.shape[0] // lax.axis_size("feat")
    start = lax.axis_index("feat") * columns
    own_half = lax.dynamic_slice_in_dim(full, start, columns, 0)
    diagonal = gram_block(full, own_half) * scale
    ahead = [from_behind(own_half, "blk", -(step + 1)) for step in range(2)]
    behind = [from_behind(own_half, "blk", step + 1) for step in range(2)]
    return jnp.stack(
        [
            gram_block(full, behind[1]) * scale,
            gram_block(full, behind[0]) * scale,
            diagonal,
            gram_block(full, ahead[0]) * scale,
            gram_block(full, ahead[1]) * scale,
        ]
    )


def solution(mesh):
    in_specs = (P("blk", "feat"),)
    out_specs = P(None, "blk", "feat")
    return jax.shard_map(local, mesh=mesh, in_specs=in_specs, out_specs=out_specs, check_vma=False)
```

profile of v0, /device:TPU:0, one launch (start us, length us, event | category | flops | bytes accessed | tf_op | source)
XLA Modules:
  0.0 248.6 jit_solution(6134391584032130311)
XLA Ops:
  0.0 2.4 copy.3
  2.4 3.1 %broadcast_in_dim.3 = f32[2,768,1024]{1,2,0:T(8,128)} broadcast(f32[768,1024]{0,1:T(8,128)S(1)} %copy.3), dimensions={1,2} | broadcast | bytes 9437184 | tf_op jit(solution)/shard_map/broadcast_in_dim | solution.py:8
  5.4 6.3 %all-to-all-start = ((f32[2,768,1024]{1,2,0:T(8,128)}), f32[2,768,1024]{1,2,0:T(8,128)}, u32[]{:S(2)}, u32[]{:S(2)}) async-start(f32[2,768,1024]{1,2,0:T(8,128)} %broadcast_in_dim.3), calls=%async_computation | async-start | bytes 12582912 | tf_op jit(solution)/shard_map/all_to_all | solution.py:9
  11.7 69.9 %all-to-all-done = f32[2,768,1024]{1,2,0:T(8,128)} async-done(((f32[2,768,1024]{1,2,0:T(8,128)}), f32[2,768,1024]{1,2,0:T(8,128)}, u32[]{:S(2)}, u32[]{:S(2)}) %all-to-all-start) | async-done | bytes 6291488 | tf_op jit(solution)/shard_map/all_to_all | solution.py:9
  81.6 2.1 constant_dynamic-slice_fusion
  83.7 1.6 collective-permute-start
  85.3 0.0 collective-permute-start.1
  85.3 6.3 %collective-permute-start.2 = (f32[384,2048]{0,1:T(8,128)S(1)}, f32[384,2048]{0,1:T(8,128)S(1)}, u32[]{:S(2)}, u32[]{:S(2)}) collective-permute-start(f32[384,2048]{0,1:T(8,128)S(1)} %constant_dynamic-slice_fusion), channel_id=1, source_target_pairs={{0,254},{2,0},{4,2},{6,4},{8,6},{10,8},{12,10},{14,12},{16,14},{18... | collective-permute-start | bytes 9437192 | tf_op jit(solution)/shard_map/ppermute | solution.py:25
  91.7 3.1 %collective-permute-start.3 = (f32[384,2048]{0,1:T(8,128)S(1)}, f32[384,2048]{0,1:T(8,128)S(1)}, u32[]{:S(2)}, u32[]{:S(2)}) collective-permute-start(f32[384,2048]{0,1:T(8,128)S(1)} %constant_dynamic-slice_fusion), channel_id=1, source_target_pairs={{0,252},{2,254},{4,0},{6,2},{8,4},{10,6},{12,8},{14,10},{16,12},{1... | collective-permute-start | bytes 9437192 | tf_op jit(solution)/shard_map/ppermute | solution.py:25
  94.7 67.1 %collective-permute-done = f32[384,2048]{0,1:T(8,128)S(1)} collective-permute-done((f32[384,2048]{0,1:T(8,128)S(1)}, f32[384,2048]{0,1:T(8,128)S(1)}, u32[]{:S(2)}, u32[]{:S(2)}) %collective-permute-start) | collective-permute-done | bytes 3145760 | tf_op jit(solution)/shard_map/ppermute | solution.py:25
  161.9 11.7 %fusion.1 = f32[5,768,384]{1,2,0:T(8,128)} fusion(f32[384,2048]{0,1:T(8,128)S(1)} %collective-permute-done, f32[768,2048]{0,1:T(8,128)} %bitcast.1), kind=kOutput, calls=%fused_computation.6 | convolution fusion | flops 7248052224 | bytes 10616832 | tf_op jit(solution)/shard_map/dot_general | solution.py:29
  173.6 20.2 %collective-permute-done.1 = f32[384,2048]{0,1:T(8,128)S(1)} collective-permute-done((f32[384,2048]{0,1:T(8,128)S(1)}, f32[384,2048]{0,1:T(8,128)S(1)}, u32[]{:S(2)}, u32[]{:S(2)}) %collective-permute-start.1) | collective-permute-done | bytes 3145760 | tf_op jit(solution)/shard_map/ppermute | solution.py:25
  193.9 11.8 %fusion.3 = f32[5,768,384]{1,2,0:T(8,128)} fusion(f32[5,768,384]{1,2,0:T(8,128)} %fusion.1, f32[384,2048]{0,1:T(8,128)S(1)} %collective-permute-done.1, f32[768,2048]{0,1:T(8,128)} %bitcast.1), kind=kOutput, calls=%fused_computation.8 | convolution fusion | flops 7248052224 | bytes 10616832 | tf_op jit(solution)/shard_map/dot_general | solution.py:29
  205.7 11.8 %fusion.5 = f32[5,768,384]{1,2,0:T(8,128)} fusion(f32[5,768,384]{1,2,0:T(8,128)} %fusion.3, f32[384,2048]{0,1:T(8,128)S(1)} %constant_dynamic-slice_fusion, f32[768,2048]{0,1:T(8,128)} %bitcast.1), kind=kOutput, calls=%fused_computation.10 | convolution fusion | flops 7248052224 | bytes 10616832 | tf_op jit(solution)/shard_map/dot_general | solution.py:29
  217.5 0.0 collective-permute-done.2
  217.5 11.7 %fusion.7 = f32[5,768,384]{1,2,0:T(8,128)} fusion(f32[5,768,384]{1,2,0:T(8,128)} %fusion.5, f32[384,2048]{0,1:T(8,128)S(1)} %collective-permute-done.2, f32[768,2048]{0,1:T(8,128)} %bitcast.1), kind=kOutput, calls=%fused_computation.12 | convolution fusion | flops 7248052224 | bytes 10616832 | tf_op jit(solution)/shard_map/dot_general | solution.py:29
  229.2 0.0 collective-permute-done.3
  229.2 11.7 %fusion.9 = f32[5,768,384]{1,2,0:T(8,128)} fusion(f32[5,768,384]{1,2,0:T(8,128)} %fusion.7, f32[384,2048]{0,1:T(8,128)S(1)} %collective-permute-done.3, f32[768,2048]{0,1:T(8,128)} %bitcast.1), kind=kOutput, calls=%fused_computation.14 | convolution fusion | flops 7248052224 | bytes 10616832 | tf_op jit(solution)/shard_map/dot_general | solution.py:29
  241.0 7.6 %copy.4 = f32[5,768,384]{2,1,0:T(8,128)} copy(f32[5,768,384]{1,2,0:T(8,128)} %fusion.9) | data formatting | bytes 11796480 | tf_op jit(solution)/shard_map/stack | solution.py:48
Async XLA Ops:
  5.4 76.2 %all-to-all-start = ((f32[2,768,1024]{1,2,0:T(8,128)}), f32[2,768,1024]{1,2,0:T(8,128)}, u32[]{:S(2)}, u32[]{:S(2)}) async-start(f32[2,768,1024]{1,2,0:T(8,128)} %broadcast_in_dim.3), calls=%async_computation | async-start | bytes 12582912 | tf_op jit(solution)/shard_map/all_to_all | solution.py:9
  83.7 78.1 %collective-permute-start = (f32[384,2048]{0,1:T(8,128)S(1)}, f32[384,2048]{0,1:T(8,128)S(1)}, u32[]{:S(2)}, u32[]{:S(2)}) collective-permute-start(f32[384,2048]{0,1:T(8,128)S(1)} %constant_dynamic-slice_fusion), channel_id=1, source_target_pairs={{0,4},{2,6},{4,8},{6,10},{8,12},{10,14},{12,16},{14,18},{16,20},{1... | collective-permute-start | bytes 9437192 | tf_op jit(solution)/shard_map/ppermute | solution.py:25
  85.3 108.5 %collective-permute-start.1 = (f32[384,2048]{0,1:T(8,128)S(1)}, f32[384,2048]{0,1:T(8,128)S(1)}, u32[]{:S(2)}, u32[]{:S(2)}) collective-permute-start(f32[384,2048]{0,1:T(8,128)S(1)} %constant_dynamic-slice_fusion), channel_id=1, source_target_pairs={{0,2},{2,4},{4,6},{6,8},{8,10},{10,12},{12,14},{14,16},{16,18},{18... | collective-permute-start | bytes 9437192 | tf_op jit(solution)/shard_map/ppermute | solution.py:25
  85.3 132.1 %collective-permute-start.2 = (f32[384,2048]{0,1:T(8,128)S(1)}, f32[384,2048]{0,1:T(8,128)S(1)}, u32[]{:S(2)}, u32[]{:S(2)}) collective-permute-start(f32[384,2048]{0,1:T(8,128)S(1)} %constant_dynamic-slice_fusion), channel_id=1, source_target_pairs={{0,254},{2,0},{4,2},{6,4},{8,6},{10,8},{12,10},{14,12},{16,14},{18... | collective-permute-start | bytes 9437192 | tf_op jit(solution)/shard_map/ppermute | solution.py:25
  91.7 137.6 %collective-permute-start.3 = (f32[384,2048]{0,1:T(8,128)S(1)}, f32[384,2048]{0,1:T(8,128)S(1)}, u32[]{:S(2)}, u32[]{:S(2)}) collective-permute-start(f32[384,2048]{0,1:T(8,128)S(1)} %constant_dynamic-slice_fusion), channel_id=1, source_target_pairs={{0,252},{2,254},{4,0},{6,2},{8,4},{10,6},{12,8},{14,10},{16,12},{1... | collective-permute-start | bytes 9437192 | tf_op jit(solution)/shard_map/ppermute | solution.py:25
where the time goes:
time: 249 us
  waiting for transfers between devices  157 us (63%)
  matrix products  58.8 us (24%)
  starting transfers between devices  17.3 us (7%)
  local copies, waits for them, and re-layouts  15.2 us (6%)
    ppermute x4, waiting for transfers between devices, from_behind(): lax.ppermute(array, axis, [(i, (i + by) % count) for i in range(count)])  87.4 us
    all_to_all x1, waiting for transfers between devices, copy_for_each(): return lax.all_to_all(copies, axis, split_axis=0, concat_axis=0, tiled=True)  69.9 us
    dot_general x5, matrix products, gram_block(): lax.dot_general(left, right, (((1,), (1,)), ((), ())), precision=lax.Prec...  58.8 us
    ppermute x4, starting transfers between devices, from_behind(): lax.ppermute(array, axis, [(i, (i + by) % count) for i in range(count)])  11 us
    another operation x1, local copies, waits for them, and re-layouts, local(): jnp.stack([gram_block(full, behind[1]) * scale, gram_block(full, behind[0...  7.65 us
    all_to_all x1, starting transfers between devices, copy_for_each(): return lax.all_to_all(copies, axis, split_axis=0, concat_axis=0, tiled=True)  6.29 us
  transfers between devices with their start and end apart: 5, of which 3 were waited for; matrix products, arithmetic and copies ran while one was open for 19% of the time, Pallas kernels for 0%

commit v1 on v0

v1 whole, which is shorter than its diff:
```python
import functools

import jax
import jax.numpy as jnp
from jax import lax
from jax.experimental import pallas as pl
from jax.experimental.pallas import tpu as pltpu
from jax.sharding import PartitionSpec as P

MESH = pl.DeviceIdType.MESH
LANES = 128
NX = 4
PARTS = 2
LEAD = 2
UP, OWN, DOWN = 0, 2, 4


def kernel(blocks, chunks, half, scale, x_ref, out_ref, buf, other, transit, r_hi, r_lo, g_hi, g_lo, r_buf, r_other, r_transit, s_sem):
    blk, f = lax.axis_index("blk"), lax.axis_index("feat")
    core = lax.rem(blk, 2)
    x = lax.rem(blk // 2, NX)
    lo = lax.rem(blk // (2 * NX), 2)
    first, last = 1 - jnp.minimum(x, 1), x // (NX - 1)
    row, plane = 2 * NX, 4 * NX

    def at(index, feat):
        return (lax.rem(index + blocks, blocks), feat)

    near = at(blk + row - 2 * row * lo, f)
    cross = at(blk + row - 2 * row * lo, 1 - f)
    twin = at(blk + 1 - 2 * core, f)
    up = at(blk + 2 - row * last + plane * last * (1 - lo), f)
    down = at(blk - 2 + row * first - plane * first * lo, f)
    up_source = at(blk - 2 + row * first - plane * first * (1 - lo), f)
    down_source = at(blk + 2 - row * last + plane * last * lo, f)
    twin_slot = 3 - 2 * core
    extra_slot = 1 + 2 * core
    passed_slot = 4 - 4 * core
    kept_slot = 4 * core
    part = half // PARTS

    def load(k):
        columns = pl.ds(k * LANES, LANES)
        mine = pl.ds(pl.multiple_of(f * half, half), half)
        rest = pl.ds(pl.multiple_of((1 - f) * half, half), half)
        return (
            pltpu.make_async_copy(x_ref.at[mine, columns], buf.at[OWN, 0, k], r_buf.at[OWN, 0, k, 0]),
            pltpu.make_async_copy(x_ref.at[rest, columns], other.at[0, k], r_other.at[0, k, 0]),
        )

    def send(flow, source, target, arrived, device):
        pltpu.make_async_remote_copy(
            src_ref=source,
            dst_ref=target,
            send_sem=s_sem.at[flow],
            recv_sem=arrived,
            device_id=device,
            device_id_type=MESH,
        ).start()

    def landed(target, arrived):
        pltpu.make_async_remote_copy(
            src_ref=target,
            dst_ref=target,
            send_sem=s_sem.at[0],
            recv_sem=arrived,
            device_id=twin,
            device_id_type=MESH,
        ).wait_recv()

    def rows(r):
        return pl.ds(r * part, part)

    def to_near(source, side, k, r):
        if side == 0:
            send(0, source, transit.at[0, k, rows(r)], r_transit.at[0, k, r], near)
        else:
            send(0, source, buf.at[OWN, 1, k, rows(r)], r_buf.at[OWN, 1, k, r], near)

    def to_cross(source, side, k, r):
        if side == 0:
            send(1, source, transit.at[1, k, rows(r)], r_transit.at[1, k, r], cross)
        else:
            send(1, source, other.at[1, k, rows(r)], r_other.at[1, k, r], cross)

    def to_up(source, side, k, r):
        send(2, source, buf.at[UP, side, k, rows(r)], r_buf.at[UP, side, k, r], up)

    def to_down(source, side, k, r):
        send(3, source, buf.at[DOWN, side, k, rows(r)], r_buf.at[DOWN, side, k, r], down)

    def to_twin(source, side, k, r):
        slot = extra_slot
        send(4, source, buf.at[slot, side, k, rows(r)], r_buf.at[slot, side, k, r], twin)

    def pass_on(side, k, r):
        slot = twin_slot
        source = buf.at[passed_slot, side, k, rows(r)]
        send(5, source, buf.at[slot, side, k, rows(r)], r_buf.at[slot, side, k, r], twin)

    def send_rows(side, k, r):
        source = buf.at[OWN, side, k, rows(r)]

        @pl.when(x < NX - 1)
        def _():
            to_up(source, side, k, r)

        @pl.when(x > 0)
        def _():
            to_down(source, side, k, r)

        to_twin(source, side, k, r)

    def wrap_rows(side, k, r):
        source = transit.at[side, k, rows(r)]

        @pl.when(x == NX - 1)
        def _():
            to_up(source, side, k, r)

        @pl.when(x == 0)
        def _():
            to_down(source, side, k, r)

    def send_own(k):
        for copy in load(k):
            copy.wait()
        for r in range(PARTS):
            to_near(buf.at[OWN, 0, k, rows(r)], 0, k, r)
            to_cross(other.at[0, k, rows(r)], 0, k, r)
            send_rows(0, k, r)

    def load_all(k, carry):
        for copy in load(k):
            copy.start()
        return carry

    lax.fori_loop(0, chunks, load_all, 0)

    barrier = pltpu.get_barrier_semaphore()
    for device in (near, cross, twin, up_source, down_source):
        pl.semaphore_signal(barrier, inc=1, device_id=device, device_id_type=MESH)
    pl.semaphore_wait(barrier, 5)

    for k in range(LEAD):
        send_own(k)

    def clear(b, carry):
        out_ref[b] = jnp.zeros(out_ref.shape[1:], jnp.float32)
        return carry

    lax.fori_loop(0, 5, clear, 0)

    def split(value):
        hi = value.astype(jnp.bfloat16)
        return hi, (value - hi.astype(jnp.float32)).astype(jnp.bfloat16)

    def dot(left, right):
        return lax.dot_general(left, right, (((1,), (1,)), ((), ())), preferred_element_type=jnp.float32)

    def multiply(k):
        for side in range(2):
            columns = pl.ds(side * LANES, LANES)
            g_hi[:, columns], g_lo[:, columns] = split(other[side, k])

        def split_slot(b, carry):
            for side in range(2):
                columns = pl.ds(side * LANES, LANES)
                r_hi[b, :, columns], r_lo[b, :, columns] = split(buf[b, side, k])
            return carry

        lax.fori_loop(0, 5, split_slot, 0)

        def block(b, carry):
            mine = pl.ds(pl.multiple_of(f * half, half), half)
            rest = pl.ds(pl.multiple_of((1 - f) * half, half), half)
            right_hi, right_lo = r_hi[b], r_lo[b]
            for where, left_hi, left_lo in ((mine, r_hi[OWN], r_lo[OWN]), (rest, g_hi[...], g_lo[...])):
                total = dot(left_hi, right_hi) + dot(left_hi, right_lo) + dot(left_lo, right_hi)
                out_ref[b, where] += total * scale
            return carry

        lax.fori_loop(0, 5, block, 0)

    def step(t, carry):
        @pl.when(t < chunks)
        def _():
            for r in range(PARTS):
                landed(transit.at[1, t, rows(r)], r_transit.at[1, t, r])
                to_near(transit.at[1, t, rows(r)], 1, t, r)
                landed(transit.at[0, t, rows(r)], r_transit.at[0, t, r])
                to_cross(transit.at[0, t, rows(r)], 1, t, r)
                wrap_rows(0, t, r)
                wrap_rows(1, t, r)

        @pl.when(jnp.logical_and(t >= 1, t <= chunks))
        def _():
            for r in range(PARTS):
                landed(buf.at[OWN, 1, t - 1, rows(r)], r_buf.at[OWN, 1, t - 1, r])
                send_rows(1, t - 1, r)

        @pl.when(t + LEAD < chunks)
        def _():
            send_own(t + LEAD)

        @pl.when(jnp.logical_and(t >= 2, t <= chunks + 1))
        def _():
            for r in range(PARTS):
                for side in range(2):
                    landed(buf.at[passed_slot, side, t - 2, rows(r)], r_buf.at[passed_slot, side, t - 2, r])
                    pass_on(side, t - 2, r)

        @pl.when(t >= 3)
        def _():
            k = t - 3
            for r in range(PARTS):
                landed(other.at[1, k, rows(r)], r_other.at[1, k, r])
                for side in range(2):
                    for slot in (kept_slot, twin_slot, extra_slot):
                        landed(buf.at[slot, side, k, rows(r)], r_buf.at[slot, side, k, r])
            multiply(k)

        return carry

    lax.fori_loop(0, chunks + 3, step, 0)

    for flow in range(6):
        pltpu.make_async_remote_copy(
            src_ref=transit,
            dst_ref=transit,
            send_sem=s_sem.at[flow],
            recv_sem=r_transit.at[0, 0, 0],
            device_id=twin,
            device_id_type=MESH,
        ).wait_send()


def local(samples):
    count, width = samples.shape
    feats = lax.axis_size("feat")
    half, chunks = count // feats, width // LANES
    scale = float(1.0 / (width * feats) ** 0.5)
    block = (half, LANES)
    return pl.pallas_call(
        functools.partial(kernel, lax.axis_size("blk"), chunks, half, scale),
        out_shape=jax.ShapeDtypeStruct((5, count, half), jnp.float32),
        in_specs=[pl.BlockSpec(memory_space=pltpu.HBM)],
        out_specs=pl.BlockSpec(memory_space=pltpu.VMEM),
        scratch_shapes=[
            pltpu.VMEM((5, 2, chunks, *block), jnp.float32),
            pltpu.VMEM((2, chunks, *block), jnp.float32),
            pltpu.VMEM((2, chunks, *block), jnp.float32),
            pltpu.VMEM((5, half, 2 * LANES), jnp.bfloat16),
            pltpu.VMEM((5, half, 2 * LANES), jnp.bfloat16),
            pltpu.VMEM((half, 2 * LANES), jnp.bfloat16),
            pltpu.VMEM((half, 2 * LANES), jnp.bfloat16),
            pltpu.SemaphoreType.DMA((5, 2, chunks, PARTS)),
            pltpu.SemaphoreType.DMA((2, chunks, PARTS)),
            pltpu.SemaphoreType.DMA((2, chunks, PARTS)),
            pltpu.SemaphoreType.DMA((6,)),
        ],
        compiler_params=pltpu.CompilerParams(collective_id=0, has_side_effects=True, vmem_limit_bytes=63 * 1024 * 1024),
        name="banded_gram",
    )(samples)


def solution(mesh):
    in_specs = (P("blk", "feat"),)
    out_specs = P(None, "blk", "feat")
    return jax.shard_map(local, mesh=mesh, in_specs=in_specs, out_specs=out_specs, check_vma=False)
```

time: 249 us -> 102 us (0.41)
  the two profiles are of different devices: /device:TPU:0 before, /device:TPU:1 now
where the time goes in v1:
time: 102 us; the launch traced here: 101 us
  Pallas kernels  95.7 us (94%)
  local copies, waits for them, and re-layouts  5.63 us (6%)
    pallas_call x1, Pallas kernels, local(): pl.pallas_call(functools.partial(kernel, lax.axis_size('blk'), chunks, ha...  95.7 us
    unnamed x1, local copies, waits for them, and re-layouts  5.63 us

profile of v1, /device:TPU:1, one launch (start us, length us, event | category | flops | bytes accessed | tf_op | source)
XLA Modules:
  0.0 101.3 jit_solution(1979762953687469454)
XLA Ops:
  0.0 95.7 %banded_gram.1 = f32[5,768,384]{2,1,0:T(8,128)} custom-call(f32[768,1024]{1,0:T(8,128)} %x_ref.1), custom_call_target="tpu_custom_call" | custom-call | tf_op jit(solution)/shard_map/banded_gram/pallas_call | solution.py:244
  95.7 5.6 %copy.3 = f32[5,768,384]{2,1,0:T(8,128)} copy(f32[5,768,384]{2,1,0:T(8,128)} %banded_gram.1) | data formatting | bytes 11796480

commit v2 on v1

v2 whole, which is shorter than its diff:
```python
import functools

import jax
import jax.numpy as jnp
from jax import lax
from jax.experimental import pallas as pl
from jax.experimental.pallas import tpu as pltpu
from jax.sharding import PartitionSpec as P

MESH = pl.DeviceIdType.MESH
LANES = 128
NX = 4
PARTS = 2
TILE = 256
ORDER = ("relay", "relay_back", "given", "pass_on", "own_near", "own_cross", "own_rows", "consume")
LATER = dict(own_near=1, own_cross=0, own_rows=1, relay=3, relay_back=4, given=6, pass_on=8, consume=9)
UP, OWN, DOWN = 0, 2, 4


def split(value):
    hi = value.astype(jnp.bfloat16)
    return hi, (value - hi.astype(jnp.float32)).astype(jnp.bfloat16)


def dot(left, right):
    return lax.dot_general(left, right, (((1,), (1,)), ((), ())), preferred_element_type=jnp.float32)


def product(l_hi, l_lo, r_hi, r_lo, where):
    right_hi, right_lo = r_hi[where], r_lo[where]
    return dot(l_hi[...], right_hi) + dot(l_lo[...], right_hi) + dot(l_hi[...], right_lo)


def tiles(width):
    return [pl.ds(start, min(TILE, width - start)) for start in range(0, width, TILE)]


def kernel(blocks, chunks, half, scale, x_ref, acc, r_hi, r_lo, l_hi, l_lo, buf, other, transit, r_buf, r_other, r_transit, s_sem):
    blk, f = lax.axis_index("blk"), lax.axis_index("feat")
    core = lax.rem(blk, 2)
    x = lax.rem(blk // 2, NX)
    lo = lax.rem(blk // (2 * NX), 2)
    first, last = 1 - jnp.minimum(x, 1), x // (NX - 1)
    row, plane = 2 * NX, 4 * NX

    def at(index, feat):
        return (lax.rem(index + blocks, blocks), feat)

    near = at(blk + row - 2 * row * lo, f)
    cross = at(blk + row - 2 * row * lo, 1 - f)
    twin = at(blk + 1 - 2 * core, f)
    up = at(blk + 2 - row * last + plane * last * (1 - lo), f)
    down = at(blk - 2 + row * first - plane * first * lo, f)
    up_source = at(blk - 2 + row * first - plane * first * (1 - lo), f)
    down_source = at(blk + 2 - row * last + plane * last * lo, f)
    twin_slot = 3 - 2 * core
    extra_slot = 1 + 2 * core
    passed_slot = 4 - 4 * core
    kept_slot = 4 * core
    part = half // PARTS

    def rows(r):
        return pl.ds(pl.multiple_of(r * part, part), part)

    def load_mine(k, r):
        source = x_ref.at[pl.ds(pl.multiple_of(f * half + r * part, part), part), pl.ds(pl.multiple_of(k * LANES, LANES), LANES)]
        return pltpu.make_async_copy(source, buf.at[OWN, 0, k, rows(r)], r_buf.at[OWN, 0, k, r])

    def load_rest(k, r):
        source = x_ref.at[pl.ds(pl.multiple_of((1 - f) * half + r * part, part), part), pl.ds(pl.multiple_of(k * LANES, LANES), LANES)]
        return pltpu.make_async_copy(source, other.at[0, k, rows(r)], r_other.at[0, k, r])

    def send(flow, source, target, arrived, device):
        pltpu.make_async_remote_copy(
            src_ref=source,
            dst_ref=target,
            send_sem=s_sem.at[flow],
            recv_sem=arrived,
            device_id=device,
            device_id_type=MESH,
        ).start()

    def landed(target, arrived):
        pltpu.make_async_remote_copy(
            src_ref=target,
            dst_ref=target,
            send_sem=s_sem.at[0],
            recv_sem=arrived,
            device_id=twin,
            device_id_type=MESH,
        ).wait_recv()

    def to_near(source, side, k, r):
        if side == 0:
            send(0, source, transit.at[0, k, rows(r)], r_transit.at[0, k, r], near)
        else:
            send(0, source, buf.at[OWN, 1, k, rows(r)], r_buf.at[OWN, 1, k, r], near)

    def to_cross(source, side, k, r):
        if side == 0:
            send(1, source, transit.at[1, k, rows(r)], r_transit.at[1, k, r], cross)
        else:
            send(1, source, other.at[1, k, rows(r)], r_other.at[1, k, r], cross)

    def to_up(source, side, k, r):
        send(2, source, buf.at[UP, side, k, rows(r)], r_buf.at[UP, side, k, r], up)

    def to_down(source, side, k, r):
        send(3, source, buf.at[DOWN, side, k, rows(r)], r_buf.at[DOWN, side, k, r], down)

    def to_twin(source, side, k, r):
        slot = extra_slot
        send(4, source, buf.at[slot, side, k, rows(r)], r_buf.at[slot, side, k, r], twin)

    def pass_on(side, k, r):
        slot = twin_slot
        source = buf.at[passed_slot, side, k, rows(r)]
        send(5, source, buf.at[slot, side, k, rows(r)], r_buf.at[slot, side, k, r], twin)

    def send_rows(side, k, r):
        source = buf.at[OWN, side, k, rows(r)]

        @pl.when(x < NX - 1)
        def _():
            to_up(source, side, k, r)

        @pl.when(x > 0)
        def _():
            to_down(source, side, k, r)

        to_twin(source, side, k, r)

    def wrap_rows(side, k, r):
        source = transit.at[side, k, rows(r)]

        @pl.when(x == NX - 1)
        def _():
            to_up(source, side, k, r)

        @pl.when(x == 0)
        def _():
            to_down(source, side, k, r)

    def load_all(q, carry):
        k, r = q // PARTS, lax.rem(q, PARTS)
        load_mine(k, r).start()
        load_rest(k, r).start()
        return carry

    lax.fori_loop(0, chunks * PARTS, load_all, 0)

    barrier = pltpu.get_barrier_semaphore()
    for device in (near, cross, twin, up_source, down_source):
        pl.semaphore_signal(barrier, inc=1, device_id=device, device_id_type=MESH)
    pl.semaphore_wait(barrier, 5)

    acc[...] = jnp.zeros_like(acc)

    def turn(name):
        return LATER[name], ORDER.index(name)

    mine_first = "own_near" if turn("own_near") < turn("own_rows") else "own_rows"

    def own_near(k, r):
        if mine_first == "own_near":
            load_mine(k, r).wait()
        to_near(buf.at[OWN, 0, k, rows(r)], 0, k, r)

    def own_rows(k, r):
        if mine_first == "own_rows":
            load_mine(k, r).wait()
        send_rows(0, k, r)

    def own_cross(k, r):
        load_rest(k, r).wait()
        to_cross(other.at[0, k, rows(r)], 0, k, r)

    def relay(k, r):
        landed(transit.at[1, k, rows(r)], r_transit.at[1, k, r])
        to_near(transit.at[1, k, rows(r)], 1, k, r)
        wrap_rows(1, k, r)

    def relay_back(k, r):
        landed(transit.at[0, k, rows(r)], r_transit.at[0, k, r])
        to_cross(transit.at[0, k, rows(r)], 1, k, r)
        wrap_rows(0, k, r)

    def given(k, r):
        landed(buf.at[OWN, 1, k, rows(r)], r_buf.at[OWN, 1, k, r])
        send_rows(1, k, r)

    def pass_on_both(k, r):
        for side in range(2):
            landed(buf.at[passed_slot, side, k, rows(r)], r_buf.at[passed_slot, side, k, r])
            pass_on(side, k, r)

    def split_chunk(k):
        mine = pl.ds(pl.multiple_of(f * half, half), half)
        rest = pl.ds(pl.multiple_of((1 - f) * half, half), half)
        for side in range(2):
            columns = pl.ds(side * LANES, LANES)
            l_hi[mine, columns], l_lo[mine, columns] = split(buf[OWN, side, k])
            l_hi[rest, columns], l_lo[rest, columns] = split(other[side, k])

        def split_slot(b, carry):
            where = pl.ds(pl.multiple_of(b * half, half), half)
            for side in range(2):
                columns = pl.ds(side * LANES, LANES)
                r_hi[where, columns], r_lo[where, columns] = split(buf[b, side, k])
            return carry

        lax.fori_loop(0, 5, split_slot, 0)

    every = tiles(acc.shape[1])
    share = -(-len(every) // PARTS)

    def consume(k, r):
        landed(other.at[1, k, rows(r)], r_other.at[1, k, r])
        for side in range(2):
            for slot in (kept_slot, twin_slot, extra_slot):
                landed(buf.at[slot, side, k, rows(r)], r_buf.at[slot, side, k, r])

        @pl.when(r == PARTS - 1)
        def _():
            split_chunk(k)

        for turn_ in range(PARTS):
            ready = jnp.logical_and(r == PARTS - 1, k < chunks - 1) if turn_ == 0 else jnp.logical_and(r == turn_ - 1, k > 0)

            @pl.when(ready)
            def _(turn_=turn_):
                for where in every[turn_ * share : (turn_ + 1) * share]:
                    acc[:, where] += product(l_hi, l_lo, r_hi, r_lo, where) * scale

    actions = dict(
        own_near=own_near,
        own_rows=own_rows,
        own_cross=own_cross,
        relay=relay,
        relay_back=relay_back,
        given=given,
        pass_on=pass_on_both,
        consume=consume,
    )
    count = chunks * PARTS

    def step(t, carry):
        for name in ORDER:
            q = t - LATER[name]

            @pl.when(jnp.logical_and(q >= 0, q < count))
            def _(name=name, q=q):
                actions[name](q // PARTS, lax.rem(q, PARTS))

        return carry

    lax.fori_loop(0, count + max(LATER.values()), step, 0)

    for flow in range(6):
        pltpu.make_async_remote_copy(
            src_ref=transit,
            dst_ref=transit,
            send_sem=s_sem.at[flow],
            recv_sem=r_transit.at[0, 0, 0],
            device_id=twin,
            device_id_type=MESH,
        ).wait_send()


def finish(half, scale, acc, r_hi, r_lo, l_hi, l_lo, out_ref, total, sem):
    copies = [pltpu.make_async_copy(total.at[:, pl.ds(b * half, half)], out_ref.at[b], sem.at[b]) for b in range(5)]
    started = 0
    for where in tiles(acc.shape[1]):
        total[:, where] = acc[:, where] + product(l_hi, l_lo, r_hi, r_lo, where) * scale
        while (started + 1) * half <= where.start + where.size:
            copies[started].start()
            started += 1
    for copy in copies:
        copy.wait()


def local(samples):
    count, width = samples.shape
    feats = lax.axis_size("feat")
    half, chunks = count // feats, width // LANES
    scale = float(1.0 / (width * feats) ** 0.5)
    block = (half, LANES)
    parts = pl.pallas_call(
        functools.partial(kernel, lax.axis_size("blk"), chunks, half, scale),
        out_shape=[
            pltpu.VMEM((count, 5 * half), jnp.float32),
            pltpu.VMEM((5 * half, 2 * LANES), jnp.bfloat16),
            pltpu.VMEM((5 * half, 2 * LANES), jnp.bfloat16),
            pltpu.VMEM((count, 2 * LANES), jnp.bfloat16),
            pltpu.VMEM((count, 2 * LANES), jnp.bfloat16),
        ],
        in_specs=[pl.BlockSpec(memory_space=pltpu.HBM)],
        out_specs=[pl.BlockSpec(memory_space=pltpu.VMEM)] * 5,
        scratch_shapes=[
            pltpu.VMEM((5, 2, chunks, *block), jnp.float32),
            pltpu.VMEM((2, chunks, *block), jnp.float32),
            pltpu.VMEM((2, chunks, *block), jnp.float32),
            pltpu.SemaphoreType.DMA((5, 2, chunks, PARTS)),
            pltpu.SemaphoreType.DMA((2, chunks, PARTS)),
            pltpu.SemaphoreType.DMA((2, chunks, PARTS)),
            pltpu.SemaphoreType.DMA((6,)),
        ],
        compiler_params=pltpu.CompilerParams(collective_id=0, has_side_effects=True, vmem_limit_bytes=54 * 1024 * 1024),
        name="banded_gram",
    )(samples)
    return pl.pallas_call(
        functools.partial(finish, half, scale),
        out_shape=jax.ShapeDtypeStruct((5, count, half), jnp.float32),
        in_specs=[pl.BlockSpec(memory_space=pltpu.VMEM)] * 5,
        out_specs=pl.BlockSpec(memory_space=pltpu.HBM),
        scratch_shapes=[pltpu.VMEM((count, 5 * half), jnp.float32), pltpu.SemaphoreType.DMA((5,))],
        compiler_params=pltpu.CompilerParams(vmem_limit_bytes=16 * 1024 * 1024),
        name="finish",
    )(*parts)


def solution(mesh):
    in_specs = (P("blk", "feat"),)
    out_specs = P(None, "blk", "feat")
    return jax.shard_map(local, mesh=mesh, in_specs=in_specs, out_specs=out_specs, check_vma=False)
```

time: 102 us -> 92.5 us (0.907)
  local copies, waits for them, and re-layouts: 5.63 us -> 0 us
  Pallas kernels: 95.7 us -> 92.3 us
    pallas_call x1, Pallas kernels: 95.7 us -> 88.3 us  [local(): pl.pallas_call(functools.partial(kernel, lax.axis_size('blk'), chunks, ha...]
    unnamed x1 -> x0, local copies, waits for them, and re-layouts: 5.63 us -> none
    pallas_call x0 -> x1, Pallas kernels: none -> 4.01 us  [local(): pl.pallas_call(functools.partial(finish, half, scale), out_shape=jax.Shap...]
where the time goes in v2:
time: 92.5 us; the launch traced here: 92.3 us
  Pallas kernels  92.3 us (100%)
    pallas_call x1, Pallas kernels, local(): pl.pallas_call(functools.partial(kernel, lax.axis_size('blk'), chunks, ha...  88.3 us
    pallas_call x1, Pallas kernels, local(): pl.pallas_call(functools.partial(finish, half, scale), out_shape=jax.Shap...  4.01 us

profile of v2, /device:TPU:1, one launch (start us, length us, event | category | flops | bytes accessed | tf_op | source)
XLA Modules:
  0.0 92.3 jit_solution(3868160332180142790)
XLA Ops:
  0.0 88.3 %banded_gram.1 = (f32[768,1920]{1,0:T(8,128)S(1)}, bf16[1920,256]{1,0:T(8,128)(2,1)S(1)}, bf16[1920,256]{1,0:T(8,128)(2,1)S(1)}, bf16[768,256]{1,0:T(8,128)(2,1)S(1)}, bf16[768,256]{1,0:T(8,128)(2,1)S(1)}) custom-call(f32[768,1024]{1,0:T(8,128)} %x_ref.1), custom_call_target="tpu_custom_call" | custom-call | tf_op jit(solution)/shard_map/banded_gram/pallas_call | solution.py:288
  88.3 4.0 %finish.1 = f32[5,768,384]{2,1,0:T(8,128)} custom-call(f32[768,1920]{1,0:T(8,128)S(1)} %get-tuple-element.10.acc, bf16[1920,256]{1,0:T(8,128)(2,1)S(1)} %get-tuple-element.11.r_hi, bf16[1920,256]{1,0:T(8,128)(2,1)S(1)} %get-tuple-element.12.r_lo, bf16[768,256]{1,0:T(8,128)(2,1)S(1)} %get-tuple-element.13.l_hi, bf16[768,256]{1,0:T(8,128)(2,1)S(1)} %get-tuple-element.14.l_lo), custom_call_target="tpu_custom_call" | custom-call | tf_op jit(solution)/shard_map/finish/pallas_call | solution.py:311

commit v3 on v2

--- a/solution.py
+++ b/solution.py
@@ -12,8 +12,8 @@
 NX = 4
 PARTS = 2
 TILE = 256
-ORDER = ("relay", "relay_back", "given", "pass_on", "own_near", "own_cross", "own_rows", "consume")
-LATER = dict(own_near=1, own_cross=0, own_rows=1, relay=3, relay_back=4, given=6, pass_on=8, consume=9)
+ORDER = ("relay", "relay_back", "wrap_late", "given", "pass_on", "clear", "own_near", "own_cross", "own_rows", "consume")
+LATER = dict(clear=4, wrap_late=6, own_near=1, own_cross=0, own_rows=1, relay=3, relay_back=4, given=6, pass_on=8, consume=9)
 UP, OWN, DOWN = 0, 2, 4
 
 
@@ -35,13 +35,20 @@
     return [pl.ds(start, min(TILE, width - start)) for start in range(0, width, TILE)]
 
 
-def kernel(blocks, chunks, half, scale, x_ref, acc, r_hi, r_lo, l_hi, l_lo, buf, other, transit, r_buf, r_other, r_transit, s_sem):
+def early_tiles(width, half):
+    clear = lambda where, b: where.start + where.size <= b * half or where.start >= (b + 1) * half
+    return [where for where in tiles(width) if clear(where, 1) and clear(where, 3)]
+
+
+def kernel(blocks, chunks, half, scale, x_ref, acc, r_hi, r_lo, l_hi, l_lo, buf, other, transit, r_buf, r_other, r_transit, s_sem, ready):
     blk, f = lax.axis_index("blk"), lax.axis_index("feat")
     core = lax.rem(blk, 2)
     x = lax.rem(blk // 2, NX)
     lo = lax.rem(blk // (2 * NX), 2)
     first, last = 1 - jnp.minimum(x, 1), x // (NX - 1)
     row, plane = 2 * NX, 4 * NX
+    crosses, crossed = first * lo, last * lo
+    late = crosses * (1 - jnp.minimum(blk // plane, 1))
 
     def at(index, feat):
         return (lax.rem(index + blocks, blocks), feat)
@@ -130,16 +137,30 @@
 
         to_twin(source, side, k, r)
 
+    def wrap_down(side, k, r):
+        to_down(transit.at[side, k, rows(r)], side, k, r)
+
+    def wait_ready(k, r, when):
+        @pl.when(jnp.logical_and(when, k * PARTS + r == 0))
+        def _():
+            pl.semaphore_wait(ready, 1)
+
     def wrap_rows(side, k, r):
-        source = transit.at[side, k, rows(r)]
-
         @pl.when(x == NX - 1)
         def _():
-            to_up(source, side, k, r)
-
-        @pl.when(x == 0)
-        def _():
-            to_down(source, side, k, r)
+            to_up(transit.at[side, k, rows(r)], side, k, r)
+
+        @pl.when(jnp.logical_and(x == 0, late == 0))
+        def _():
+            wrap_down(side, k, r)
+
+    def wrap_late(k, r):
+        wait_ready(k, r, late == 1)
+
+        @pl.when(late == 1)
+        def _():
+            for side in range(2):
+                wrap_down(side, k, r)
 
     def load_all(q, carry):
         k, r = q // PARTS, lax.rem(q, PARTS)
@@ -150,16 +171,37 @@
     lax.fori_loop(0, chunks * PARTS, load_all, 0)
 
     barrier = pltpu.get_barrier_semaphore()
-    for device in (near, cross, twin, up_source, down_source):
+    def greet(device):
         pl.semaphore_signal(barrier, inc=1, device_id=device, device_id_type=MESH)
-    pl.semaphore_wait(barrier, 5)
-
-    acc[...] = jnp.zeros_like(acc)
+
+    for device in (near, cross, twin, up_source):
+        greet(device)
+
+    @pl.when(crossed == 0)
+    def _():
+        greet(down_source)
+
+    @pl.when(crosses == 1)
+    def _():
+        greet(down)
+
+    pl.semaphore_wait(barrier, 5 - crosses + crossed)
+
+    @pl.when(crossed == 1)
+    def _():
+        pl.semaphore_signal(ready, inc=1, device_id=down_source, device_id_type=MESH)
 
     def turn(name):
         return LATER[name], ORDER.index(name)
 
+    wrap_first = "relay" if turn("relay") < turn("relay_back") else "relay_back"
+    in_time = jnp.logical_and(crosses == 1, late == 0)
     mine_first = "own_near" if turn("own_near") < turn("own_rows") else "own_rows"
+
+    def clear(k, r):
+        @pl.when(k * PARTS + r == 0)
+        def _():
+            acc[...] = jnp.zeros_like(acc)
 
     def own_near(k, r):
         if mine_first == "own_near":
@@ -178,11 +220,15 @@
     def relay(k, r):
         landed(transit.at[1, k, rows(r)], r_transit.at[1, k, r])
         to_near(transit.at[1, k, rows(r)], 1, k, r)
+        if wrap_first == "relay":
+            wait_ready(k, r, in_time)
         wrap_rows(1, k, r)
 
     def relay_back(k, r):
         landed(transit.at[0, k, rows(r)], r_transit.at[0, k, r])
         to_cross(transit.at[0, k, rows(r)], 1, k, r)
+        if wrap_first == "relay_back":
+            wait_ready(k, r, in_time)
         wrap_rows(0, k, r)
 
     def given(k, r):
@@ -194,7 +240,7 @@
             landed(buf.at[passed_slot, side, k, rows(r)], r_buf.at[passed_slot, side, k, r])
             pass_on(side, k, r)
 
-    def split_chunk(k):
+    def split_left(k):
         mine = pl.ds(pl.multiple_of(f * half, half), half)
         rest = pl.ds(pl.multiple_of((1 - f) * half, half), half)
         for side in range(2):
@@ -202,35 +248,59 @@
             l_hi[mine, columns], l_lo[mine, columns] = split(buf[OWN, side, k])
             l_hi[rest, columns], l_lo[rest, columns] = split(other[side, k])
 
-        def split_slot(b, carry):
-            where = pl.ds(pl.multiple_of(b * half, half), half)
-            for side in range(2):
-                columns = pl.ds(side * LANES, LANES)
-                r_hi[where, columns], r_lo[where, columns] = split(buf[b, side, k])
+    def split_slot(b, k):
+        where = pl.ds(pl.multiple_of(b * half, half), half)
+        for side in range(2):
+            columns = pl.ds(side * LANES, LANES)
+            r_hi[where, columns], r_lo[where, columns] = split(buf[b, side, k])
+
+    def split_slots(k):
+        def one(b, carry):
+            @pl.when(b != extra_slot)
+            def _():
+                split_slot(b, k)
+
             return carry
 
-        lax.fori_loop(0, 5, split_slot, 0)
+        lax.fori_loop(0, 5, one, 0)
 
     every = tiles(acc.shape[1])
     share = -(-len(every) // PARTS)
+    early = early_tiles(acc.shape[1], half)
+
+    def add(wheres):
+        for where in wheres:
+            acc[:, where] += product(l_hi, l_lo, r_hi, r_lo, where) * scale
 
     def consume(k, r):
+        complete = r == PARTS - 1
         landed(other.at[1, k, rows(r)], r_other.at[1, k, r])
         for side in range(2):
-            for slot in (kept_slot, twin_slot, extra_slot):
+            for slot in (kept_slot, twin_slot):
                 landed(buf.at[slot, side, k, rows(r)], r_buf.at[slot, side, k, r])
 
-        @pl.when(r == PARTS - 1)
-        def _():
-            split_chunk(k)
+        @pl.when(complete)
+        def _():
+            split_left(k)
+            split_slots(k)
+
+        @pl.when(jnp.logical_and(complete, k == chunks - 1))
+        def _():
+            add(early)
+
+        for side in range(2):
+            landed(buf.at[extra_slot, side, k, rows(r)], r_buf.at[extra_slot, side, k, r])
+
+        @pl.when(complete)
+        def _():
+            split_slot(extra_slot, k)
 
         for turn_ in range(PARTS):
-            ready = jnp.logical_and(r == PARTS - 1, k < chunks - 1) if turn_ == 0 else jnp.logical_and(r == turn_ - 1, k > 0)
-
-            @pl.when(ready)
+            ready_ = jnp.logical_and(complete, k < chunks - 1) if turn_ == 0 else jnp.logical_and(r == turn_ - 1, k > 0)
+
+            @pl.when(ready_)
             def _(turn_=turn_):
-                for where in every[turn_ * share : (turn_ + 1) * share]:
-                    acc[:, where] += product(l_hi, l_lo, r_hi, r_lo, where) * scale
+                add(every[turn_ * share : (turn_ + 1) * share])
 
     actions = dict(
         own_near=own_near,
@@ -238,9 +308,11 @@
         own_cross=own_cross,
         relay=relay,
         relay_back=relay_back,
+        wrap_late=wrap_late,
         given=given,
         pass_on=pass_on_both,
         consume=consume,
+        clear=clear,
     )
     count = chunks * PARTS
 
@@ -268,13 +340,25 @@
 
 
 def finish(half, scale, acc, r_hi, r_lo, l_hi, l_lo, out_ref, total, sem):
-    copies = [pltpu.make_async_copy(total.at[:, pl.ds(b * half, half)], out_ref.at[b], sem.at[b]) for b in range(5)]
-    started = 0
-    for where in tiles(acc.shape[1]):
-        total[:, where] = acc[:, where] + product(l_hi, l_lo, r_hi, r_lo, where) * scale
-        while (started + 1) * half <= where.start + where.size:
-            copies[started].start()
-            started += 1
+    every = tiles(acc.shape[1])
+    early = early_tiles(acc.shape[1], half)
+    copies = []
+
+    def write(source, where):
+        for b in range(5):
+            start, stop = max(where.start, b * half), min(where.start + where.size, (b + 1) * half)
+            if start < stop:
+                target = out_ref.at[b, :, pl.ds(start - b * half, stop - start)]
+                copies.append(pltpu.make_async_copy(source.at[:, pl.ds(start, stop - start)], target, sem.at[len(copies)]))
+                copies[-1].start()
+
+    for where in every:
+        if where in early:
+            write(acc, where)
+    for where in every:
+        if where not in early:
+            total[:, where] = acc[:, where] + product(l_hi, l_lo, r_hi, r_lo, where) * scale
+            write(total, where)
     for copy in copies:
         copy.wait()
 
@@ -304,6 +388,7 @@
             pltpu.SemaphoreType.DMA((2, chunks, PARTS)),
             pltpu.SemaphoreType.DMA((2, chunks, PARTS)),
             pltpu.SemaphoreType.DMA((6,)),
+            pltpu.SemaphoreType.REGULAR,
         ],
         compiler_params=pltpu.CompilerParams(collective_id=0, has_side_effects=True, vmem_limit_bytes=54 * 1024 * 1024),
         name="banded_gram",
@@ -313,7 +398,7 @@
         out_shape=jax.ShapeDtypeStruct((5, count, half), jnp.float32),
         in_specs=[pl.BlockSpec(memory_space=pltpu.VMEM)] * 5,
         out_specs=pl.BlockSpec(memory_space=pltpu.HBM),
-        scratch_shapes=[pltpu.VMEM((count, 5 * half), jnp.float32), pltpu.SemaphoreType.DMA((5,))],
+        scratch_shapes=[pltpu.VMEM((count, 5 * half), jnp.float32), pltpu.SemaphoreType.DMA((16,))],
         compiler_params=pltpu.CompilerParams(vmem_limit_bytes=16 * 1024 * 1024),
         name="finish",
     )(*parts)

time: 92.5 us -> 91.5 us (0.989)
    pallas_call x1, Pallas kernels: 4.01 us -> 2.81 us  [local(): pl.pallas_call(functools.partial(finish, half, scale), out_shape=jax.Shap...]
where the time goes in v3:
time: 91.5 us; the launch traced here: 91.4 us
  Pallas kernels  91.4 us (100%)
    pallas_call x1, Pallas kernels, local(): pl.pallas_call(functools.partial(kernel, lax.axis_size('blk'), chunks, ha...  88.6 us
    pallas_call x1, Pallas kernels, local(): pl.pallas_call(functools.partial(finish, half, scale), out_shape=jax.Shap...  2.81 us

profile of v3, /device:TPU:1, one launch (start us, length us, event | category | flops | bytes accessed | tf_op | source)
XLA Modules:
  0.0 91.4 jit_solution(7651052917815250070)
XLA Ops:
  0.0 88.6 %banded_gram.1 = (f32[768,1920]{1,0:T(8,128)S(1)}, bf16[1920,256]{1,0:T(8,128)(2,1)S(1)}, bf16[1920,256]{1,0:T(8,128)(2,1)S(1)}, bf16[768,256]{1,0:T(8,128)(2,1)S(1)}, bf16[768,256]{1,0:T(8,128)(2,1)S(1)}) custom-call(f32[768,1024]{1,0:T(8,128)} %x_ref.1), custom_call_target="tpu_custom_call" | custom-call | tf_op jit(solution)/shard_map/banded_gram/pallas_call | solution.py:372
  88.6 2.8 %finish.1 = f32[5,768,384]{2,1,0:T(8,128)} custom-call(f32[768,1920]{1,0:T(8,128)S(1)} %get-tuple-element.10.acc, bf16[1920,256]{1,0:T(8,128)(2,1)S(1)} %get-tuple-element.11.r_hi, bf16[1920,256]{1,0:T(8,128)(2,1)S(1)} %get-tuple-element.12.r_lo, bf16[768,256]{1,0:T(8,128)(2,1)S(1)} %get-tuple-element.13.l_hi, bf16[768,256]{1,0:T(8,128)(2,1)S(1)} %get-tuple-element.14.l_lo), custom_call_target="tpu_custom_call" | custom-call | tf_op jit(solution)/shard_map/finish/pallas_call | solution.py:396

commit v4 on v3

--- a/solution.py
+++ b/solution.py
@@ -13,7 +13,7 @@
 PARTS = 2
 TILE = 256
 ORDER = ("relay", "relay_back", "wrap_late", "given", "pass_on", "clear", "own_near", "own_cross", "own_rows", "consume")
-LATER = dict(clear=4, wrap_late=6, own_near=1, own_cross=0, own_rows=1, relay=3, relay_back=4, given=6, pass_on=8, consume=9)
+LATER = dict(own_near=1, own_cross=0, own_rows=1, relay=2, relay_back=3, wrap_late=5, given=4, pass_on=6, consume=7, clear=4)
 UP, OWN, DOWN = 0, 2, 4
 
 
@@ -168,8 +168,6 @@
         load_rest(k, r).start()
         return carry
 
-    lax.fori_loop(0, chunks * PARTS, load_all, 0)
-
     barrier = pltpu.get_barrier_semaphore()
     def greet(device):
         pl.semaphore_signal(barrier, inc=1, device_id=device, device_id_type=MESH)
@@ -184,6 +182,8 @@
     @pl.when(crosses == 1)
     def _():
         greet(down)
+
+    lax.fori_loop(0, chunks * PARTS, load_all, 0)
 
     pl.semaphore_wait(barrier, 5 - crosses + crossed)
 

time: 91.5 us -> 91.9 us (level)
  no operation moved by 1% of the time
where the time goes in v4:
time: 91.9 us
  Pallas kernels  91.9 us (100%)
    pallas_call x1, Pallas kernels, local(): pl.pallas_call(functools.partial(kernel, lax.axis_size('blk'), chunks, ha...  89.1 us
    pallas_call x1, Pallas kernels, local(): pl.pallas_call(functools.partial(finish, half, scale), out_shape=jax.Shap...  2.81 us

profile of v4, /device:TPU:1, one launch (start us, length us, event | category | flops | bytes accessed | tf_op | source)
XLA Modules:
  0.0 91.9 jit_solution(15745749930966321532)
XLA Ops:
  0.0 89.1 %banded_gram.1 = (f32[768,1920]{1,0:T(8,128)S(1)}, bf16[1920,256]{1,0:T(8,128)(2,1)S(1)}, bf16[1920,256]{1,0:T(8,128)(2,1)S(1)}, bf16[768,256]{1,0:T(8,128)(2,1)S(1)}, bf16[768,256]{1,0:T(8,128)(2,1)S(1)}) custom-call(f32[768,1024]{1,0:T(8,128)} %x_ref.1), custom_call_target="tpu_custom_call" | custom-call | tf_op jit(solution)/shard_map/banded_gram/pallas_call | solution.py:372
  89.1 2.8 %finish.1 = f32[5,768,384]{2,1,0:T(8,128)} custom-call(f32[768,1920]{1,0:T(8,128)S(1)} %get-tuple-element.10.acc, bf16[1920,256]{1,0:T(8,128)(2,1)S(1)} %get-tuple-element.11.r_hi, bf16[1920,256]{1,0:T(8,128)(2,1)S(1)} %get-tuple-element.12.r_lo, bf16[768,256]{1,0:T(8,128)(2,1)S(1)} %get-tuple-element.13.l_hi, bf16[768,256]{1,0:T(8,128)(2,1)S(1)} %get-tuple-element.14.l_lo), custom_call_target="tpu_custom_call" | custom-call | tf_op jit(solution)/shard_map/finish/pallas_call | solution.py:396
